TPU v7x, 32 devices: a whole 2x2x4 slice. The times are simulated.
32 devices in a mesh: grid: 8 (over z, y), band: 4 (over x, core).
Axes of the slice: x: 2, y: 2, z: 4, core: 2. Of those that a mesh axis runs over, the one named last changes fastest.
Arguments:
- orbitals: float32 [32, 16, 16, 512], P('grid', None, None, 'band'), may hold values from -80 to 80
- projectors: float32 [32, 16, 16, 512], P('grid', None, None, 'band'), may hold values from -0.09375 to 0.09375
- potential: float32 [32, 16, 16], P('grid'), may hold values from 0.3 to 3
Outputs:
- updated_orbitals: float32 [32, 16, 16, 512], P('grid', None, None, 'band')
- rayleigh_quotients: float32 [3, 512], P(None, 'band')
- residual_norms: float32 [3, 512], P(None, 'band')
All inputs are finite; a program needn't handle non-finite values.
Results may differ from a plain program's by a relative error of at most 0.00012.
Values sent between devices are 32-bit elements; how exact they have to be, the bound alone decides.
A program may use at most 128 MiB of HBM per device.

v0:
```python
import jax
import jax.numpy as jnp
from jax import lax
from jax.sharding import PartitionSpec as P

ITERS = 3
STENCIL = (-205.0 / 72.0, 8.0 / 5.0, -1.0 / 5.0, 8.0 / 315.0, -1.0 / 560.0)
STEP_LENGTH = 0.25
NORM_EPS = 1e-06
HIGHEST = lax.Precision.HIGHEST


def with_halo(block, sides, width):
    for axis, dim in sides:
        count = lax.axis_size(axis)
        forward = [(i, i + 1) for i in range(count - 1)]
        forward.append((count - 1, 0))
        backward = [(target, source) for source, target in forward]
        low = lax.ppermute(
            lax.slice_in_dim(block, block.shape[dim] - width, None, axis=dim), axis, forward
        )
        high = lax.ppermute(lax.slice_in_dim(block, 0, width, axis=dim), axis, backward)
        block = jnp.concatenate([low, block, high], axis=dim)
    return block


def matmul(left, right):
    return jnp.dot(left, right, precision=HIGHEST, preferred_element_type=jnp.float32)


def laplacian(grid_field):
    padded = with_halo(grid_field, (("grid", 0),), 4)
    planes_here = grid_field.shape[0]
    result = 3.0 * STENCIL[0] * grid_field
    for distance in range(1, 5):
        result = result + STENCIL[distance] * (
            padded[4 + distance : 4 + distance + planes_here]
            + padded[4 - distance : 4 - distance + planes_here]
        )
    for dimension in (1, 2):
        for distance in range(1, 5):
            result = result + STENCIL[distance] * (
                jnp.roll(grid_field, distance, dimension)
                + jnp.roll(grid_field, -distance, dimension)
            )
    return result


def local(orbitals, projectors, potential):
    grid_shape = orbitals.shape
    local_bands = orbitals.shape[3]
    total_bands = local_bands * lax.axis_size("band")
    first_band = lax.axis_index("band") * local_bands
    vectors = orbitals.reshape(-1, local_bands)
    every_projector = lax.all_gather(projectors, "band", axis=3, tiled=True).reshape(
        -1, projectors.shape[3] * lax.axis_size("band")
    )
    identity_matrix = jnp.eye(total_bands, dtype=jnp.float32)
    quotient_list = []
    norm_list = []
    for iteration in range(ITERS):
        gathered = lax.all_gather(vectors.reshape(grid_shape), "band", axis=3, tiled=True).reshape(
            -1, total_bands
        )
        margin = lax.psum(matmul(gathered.T, gathered), "grid")
        factor = jnp.linalg.cholesky(margin)
        inverse = jax.scipy.linalg.solve_triangular(factor, identity_matrix, lower=True)
        transform = inverse.T
        vectors = matmul(gathered, lax.dynamic_slice_in_dim(transform, first_band, local_bands, 1))
        coupling = lax.psum(matmul(every_projector.T, vectors), "grid")
        exchange_part = matmul(every_projector, coupling)
        grid_field = vectors.reshape(grid_shape)
        applied = (-0.5 * laplacian(grid_field) + potential[..., None] * grid_field).reshape(
            -1, local_bands
        ) - exchange_part
        rayleigh = lax.psum(jnp.sum(vectors * applied, axis=0), "grid")
        residual = applied - rayleigh[None, :] * vectors
        squared = lax.psum(jnp.sum(residual * residual, axis=0), "grid")
        vectors = vectors - STEP_LENGTH * residual / jnp.sqrt(squared + NORM_EPS)[None, :]
        quotient_list.append(rayleigh)
        norm_list.append(jnp.sqrt(squared))
    return (vectors.reshape(grid_shape), jnp.stack(quotient_list), jnp.stack(norm_list))


def solution(mesh):
    return jax.shard_map(
        local,
        mesh=mesh,
        in_specs=(
            P("grid", None, None, "band"),
            P("grid", None, None, "band"),
            P("grid", None, None),
        ),
        out_specs=(P("grid", None, None, "band"), P(None, "band"), P(None, "band")),
        check_vma=False,
    )
```

profile of v0, /device:TPU:0, one launch (start us, length us, event | category | flops | bytes accessed | tf_op | source)
XLA Modules:
  0.0 1202.1 jit_solution(3516485684897773808)
XLA Ops:
  7.9 27.1 %all-gather.5.cloned.1.call-done = f32[4,16,16,512]{3,2,1,0:T(8,128)} async-done(((f32[4,16,16,128]{3,2,1,0:T(8,128)}), f32[4,16,16,512]{3,2,1,0:T(8,128)}) %all-gather.5.cloned.1.call-update) | async-done | bytes 2097168 | tf_op jit(solution)/shard_map/all_gather | solution.py:62
  43.0 77.3 %all-reduce.8.cloned.1.call-done = f32[512,512]{0,1:T(8,128)} async-done(((f32[512,512]{0,1:T(8,128)}), f32[512,512]{0,1:T(8,128)}) %all-reduce.8.cloned.1.call-update) | async-done | bytes 1048592 | tf_op jit(solution)/shard_map/psum | solution.py:65
  218.7 39.3 %custom-call.34 = f32[4,128,128]{1,2,0:T(8,128)S(1)} custom-call(f32[4,128,128]{2,1,0:T(8,128)S(1)} %get-tuple-element.25), custom_call_target="InvertDiagBlocksLowerTriangular" | custom-call | tf_op jit(solution)/shard_map/jit(_solve_triangular)/triangular_solve | solution.py:67
  296.4 58.0 %all-reduce.10.cloned.1.call-done = f32[512,128]{0,1:T(8,128)} async-done(((f32[512,128]{0,1:T(8,128)}), f32[512,128]{0,1:T(8,128)}) %all-reduce.10.cloned.1.call-update) | async-done | bytes 262160 | tf_op jit(solution)/shard_map/psum | solution.py:70
  357.9 19.6 %psum.86 = f32[128]{0:T(128)S(1)} all-reduce(f32[128]{0:T(128)S(1)} %get-tuple-element.195), channel_id=1, replica_groups=mesh['grid'=8,'band'=4] {'grid'}, use_global_device_ids=true, to_apply=%region_11.14 | all-reduce | flops 128 | bytes 1024 | tf_op jit(solution)/shard_map/psum | solution.py:76
  377.8 17.1 %psum.87 = f32[128]{0:T(128)S(1)} all-reduce(f32[128]{0:T(128)S(1)} %multiply_reduce_fusion.4), channel_id=1, replica_groups=mesh['grid'=8,'band'=4] {'grid'}, use_global_device_ids=true, to_apply=%region_13.16 | all-reduce | flops 128 | bytes 1024 | tf_op jit(solution)/shard_map/psum | solution.py:78
  398.0 21.6 %all-gather.9.cloned.1.call-done = f32[4,16,16,512]{3,2,1,0:T(8,128)} async-done(((f32[4,16,16,128]{3,2,1,0:T(8,128)}), f32[4,16,16,512]{3,2,1,0:T(8,128)}) %all-gather.9.cloned.1.call-update) | async-done | bytes 2097168 | tf_op jit(solution)/shard_map/all_gather | solution.py:62
  426.8 77.9 %all-reduce.12.cloned.1.call-done = f32[512,512]{0,1:T(8,128)} async-done(((f32[512,512]{0,1:T(8,128)}), f32[512,512]{0,1:T(8,128)}) %all-reduce.12.cloned.1.call-update) | async-done | bytes 1048592 | tf_op jit(solution)/shard_map/psum | solution.py:65
  584.6 11.7 cholesky.503
  602.6 11.8 while.7
  615.1 40.1 %custom-call.38 = f32[4,128,128]{1,2,0:T(8,128)S(1)} custom-call(f32[4,128,128]{2,1,0:T(8,128)} %copy-done.45), custom_call_target="InvertDiagBlocksLowerTriangular" | custom-call | tf_op jit(solution)/shard_map/jit(_solve_triangular)/triangular_solve | solution.py:67
  680.7 14.4 %collective-permute-done.2 = f32[4,16,16,128]{3,2,1,0:T(8,128)} collective-permute-done((f32[4,16,16,128]{3,2,1,0:T(8,128)S(1)}, f32[4,16,16,128]{3,2,1,0:T(8,128)}, u32[]{:S(2)}, u32[]{:S(2)}) %collective-permute-start.2) | collective-permute-done | bytes 524320 | tf_op jit(solution)/shard_map/ppermute | solution.py:22
  701.9 51.0 %all-reduce.14.cloned.1.call-done = f32[512,128]{0,1:T(8,128)} async-done(((f32[512,128]{0,1:T(8,128)}), f32[512,128]{0,1:T(8,128)}) %all-reduce.14.cloned.1.call-update) | async-done | bytes 262160 | tf_op jit(solution)/shard_map/psum | solution.py:70
  756.4 19.6 %psum.90 = f32[128]{0:T(128)S(1)} all-reduce(f32[128]{0:T(128)S(1)} %get-tuple-element.199), channel_id=1, replica_groups=mesh['grid'=8,'band'=4] {'grid'}, use_global_device_ids=true, to_apply=%region_17.20 | all-reduce | flops 128 | bytes 1024 | tf_op jit(solution)/shard_map/psum | solution.py:76
  776.2 17.1 %psum.91 = f32[128]{0:T(128)S(1)} all-reduce(f32[128]{0:T(128)S(1)} %multiply_reduce_fusion.2), channel_id=1, replica_groups=mesh['grid'=8,'band'=4] {'grid'}, use_global_device_ids=true, to_apply=%region_19.22 | all-reduce | flops 128 | bytes 1024 | tf_op jit(solution)/shard_map/psum | solution.py:78
  797.0 21.6 %all-gather.11.cloned.1.call-done = f32[4,16,16,512]{3,2,1,0:T(8,128)} async-done(((f32[4,16,16,128]{3,2,1,0:T(8,128)}), f32[4,16,16,512]{3,2,1,0:T(8,128)}) %all-gather.11.cloned.1.call-update) | async-done | bytes 2097168 | tf_op jit(solution)/shard_map/all_gather | solution.py:62
  825.5 78.3 %all-reduce.16.cloned.1.call-done = f32[512,512]{0,1:T(8,128)} async-done(((f32[512,512]{0,1:T(8,128)}), f32[512,512]{0,1:T(8,128)}) %all-reduce.16.cloned.1.call-update) | async-done | bytes 1048592 | tf_op jit(solution)/shard_map/psum | solution.py:65
  983.7 11.7 cholesky.575
  1001.9 11.8 while.8
  1014.4 40.1 %custom-call.42 = f32[4,128,128]{1,2,0:T(8,128)S(1)} custom-call(f32[4,128,128]{2,1,0:T(8,128)} %copy-done.44), custom_call_target="InvertDiagBlocksLowerTriangular" | custom-call | tf_op jit(solution)/shard_map/jit(_solve_triangular)/triangular_solve | solution.py:67
  1079.6 14.8 %collective-permute-done.4 = f32[4,16,16,128]{3,2,1,0:T(8,128)} collective-permute-done((f32[4,16,16,128]{3,2,1,0:T(8,128)S(1)}, f32[4,16,16,128]{3,2,1,0:T(8,128)}, u32[]{:S(2)}, u32[]{:S(2)}) %collective-permute-start.4) | collective-permute-done | bytes 524320 | tf_op jit(solution)/shard_map/ppermute | solution.py:22
  1101.2 51.0 %all-reduce.18.cloned.1.call-done = f32[512,128]{0,1:T(8,128)} async-done(((f32[512,128]{0,1:T(8,128)}), f32[512,128]{0,1:T(8,128)}) %all-reduce.18.cloned.1.call-update) | async-done | bytes 262160 | tf_op jit(solution)/shard_map/psum | solution.py:70
  1155.7 19.6 %psum.94 = f32[128]{0:T(128)S(1)} all-reduce(f32[128]{0:T(128)S(1)} %get-tuple-element.203), channel_id=1, replica_groups=mesh['grid'=8,'band'=4] {'grid'}, use_global_device_ids=true, to_apply=%region_23.26 | all-reduce | flops 128 | bytes 1024 | tf_op jit(solution)/shard_map/psum | solution.py:76
  1175.5 17.1 %psum.95 = f32[128]{0:T(128)S(1)} all-reduce(f32[128]{0:T(128)S(1)} %multiply_reduce_fusion), channel_id=1, replica_groups=mesh['grid'=8,'band'=4] {'grid'}, use_global_device_ids=true, to_apply=%region_25.28 | all-reduce | flops 128 | bytes 1024 | tf_op jit(solution)/shard_map/psum | solution.py:78
  (353 shorter events, 440.8 us)
Async XLA Ops:
  7.2 27.9 %all-gather.5.cloned.1.call-start = ((), (), s32[]{:S(2)}) async-start(), calls=%async_computation | async-start | bytes 2621440 | tf_op jit(solution)/shard_map/all_gather | solution.py:62
  7.9 112.4 %all-reduce.8.cloned.1.call-start = ((), (), s32[]{:S(2)}) async-start(), calls=%async_computation.1 | async-start | bytes 2097152 | tf_op jit(solution)/shard_map/psum | solution.py:65
  41.8 236.4 %all-gather.7.cloned.1.call-start = ((), (), s32[]{:S(2)}) async-start(), calls=%async_computation.2 | async-start | bytes 2621440 | tf_op jit(solution)/shard_map/all_gather | solution.py:55
  42.5 311.9 %all-reduce.10.cloned.1.call-start = ((), (), s32[]{:S(2)}) async-start(), calls=%async_computation.3 | async-start | bytes 524288 | tf_op jit(solution)/shard_map/psum | solution.py:70
  43.0 217.1 %copy-start.4 = (f32[512,512]{1,0:T(8,128)}, f32[512,512]{1,0:T(8,128)S(1)}, u32[]{:S(2)}) copy-start(f32[512,512]{1,0:T(8,128)S(1)} %fusion.6) | copy-start | bytes 3145732
  263.7 24.9 %collective-permute-start = (f32[4,16,16,128]{3,2,1,0:T(8,128)S(1)}, f32[4,16,16,128]{3,2,1,0:T(8,128)S(1)}, u32[]{:S(2)}, u32[]{:S(2)}) collective-permute-start(f32[4,16,16,128]{3,2,1,0:T(8,128)S(1)} %bitcast.253), channel_id=1, source_target_pairs={{4,0},{8,4},{12,8},{16,12},{20,16},{24,20},{28,24},{0,28},{5,1},{9... | collective-permute-start | bytes 1572872 | tf_op jit(solution)/shard_map/ppermute | solution.py:22
  266.7 21.9 %collective-permute-start.1 = (f32[4,16,16,128]{3,2,1,0:T(8,128)S(1)}, f32[4,16,16,128]{3,2,1,0:T(8,128)S(1)}, u32[]{:S(2)}, u32[]{:S(2)}) collective-permute-start(f32[4,16,16,128]{3,2,1,0:T(8,128)S(1)} %bitcast.254), channel_id=1, source_target_pairs={{0,4},{4,8},{8,12},{12,16},{16,20},{20,24},{24,28},{28,0},{1,5},{5... | collective-permute-start | bytes 1572872 | tf_op jit(solution)/shard_map/ppermute | solution.py:19
  281.8 137.8 %all-gather.9.cloned.1.call-start = ((), (), s32[]{:S(2)}) async-start(), calls=%async_computation.4 | async-start | bytes 2621440 | tf_op jit(solution)/shard_map/all_gather | solution.py:62
  289.6 64.8 %copy-start = (f32[4,16,16,512]{3,2,1,0:T(8,128)S(1)}, f32[4,16,16,512]{3,2,1,0:T(8,128)}, u32[]{:S(2)}) copy-start(f32[4,16,16,512]{3,2,1,0:T(8,128)} %all-gather.7.cloned.1.call-done) | copy-start | bytes 6291460
  398.0 106.8 %all-reduce.12.cloned.1.call-start = ((), (), s32[]{:S(2)}) async-start(), calls=%async_computation.5 | async-start | bytes 2097152 | tf_op jit(solution)/shard_map/psum | solution.py:65
  426.3 326.6 %all-reduce.14.cloned.1.call-start = ((), (), s32[]{:S(2)}) async-start(), calls=%async_computation.6 | async-start | bytes 524288 | tf_op jit(solution)/shard_map/psum | solution.py:70
  559.6 95.7 %copy-start.5 = (f32[512,512]{1,0:T(8,128)S(1)}, f32[512,512]{1,0:T(8,128)}, u32[]{:S(2)}) copy-start(f32[512,512]{1,0:T(8,128)} %copy-done.4) | copy-start | bytes 3145732
  669.1 26.0 %collective-permute-start.2 = (f32[4,16,16,128]{3,2,1,0:T(8,128)S(1)}, f32[4,16,16,128]{3,2,1,0:T(8,128)}, u32[]{:S(2)}, u32[]{:S(2)}) collective-permute-start(f32[4,16,16,128]{3,2,1,0:T(8,128)S(1)} %bitcast.221), channel_id=1, source_target_pairs={{4,0},{8,4},{12,8},{16,12},{20,16},{24,20},{28,24},{0,28},{5,1},{9... | collective-permute-start | bytes 1572872 | tf_op jit(solution)/shard_map/ppermute | solution.py:22
  672.0 23.1 %collective-permute-start.3 = (f32[4,16,16,128]{3,2,1,0:T(8,128)S(1)}, f32[4,16,16,128]{3,2,1,0:T(8,128)}, u32[]{:S(2)}, u32[]{:S(2)}) collective-permute-start(f32[4,16,16,128]{3,2,1,0:T(8,128)S(1)} %bitcast.222), channel_id=1, source_target_pairs={{0,4},{4,8},{8,12},{12,16},{16,20},{20,24},{24,28},{28,0},{1,5},{5... | collective-permute-start | bytes 1572872 | tf_op jit(solution)/shard_map/ppermute | solution.py:19
  680.0 138.6 %all-gather.11.cloned.1.call-start = ((), (), s32[]{:S(2)}) async-start(), calls=%async_computation.7 | async-start | bytes 2621440 | tf_op jit(solution)/shard_map/all_gather | solution.py:62
  796.9 106.8 %all-reduce.16.cloned.1.call-start = ((), (), s32[]{:S(2)}) async-start(), calls=%async_computation.8 | async-start | bytes 2097152 | tf_op jit(solution)/shard_map/psum | solution.py:65
  825.3 326.9 %all-reduce.18.cloned.1.call-start = ((), (), s32[]{:S(2)}) async-start(), calls=%async_computation.9 | async-start | bytes 524288 | tf_op jit(solution)/shard_map/psum | solution.py:70
  958.7 95.8 %copy-start.6 = (f32[512,512]{1,0:T(8,128)S(1)}, f32[512,512]{1,0:T(8,128)}, u32[]{:S(2)}) copy-start(f32[512,512]{1,0:T(8,128)} %copy-done.4) | copy-start | bytes 3145732
  1068.4 26.0 %collective-permute-start.4 = (f32[4,16,16,128]{3,2,1,0:T(8,128)S(1)}, f32[4,16,16,128]{3,2,1,0:T(8,128)}, u32[]{:S(2)}, u32[]{:S(2)}) collective-permute-start(f32[4,16,16,128]{3,2,1,0:T(8,128)S(1)} %bitcast.240), channel_id=1, source_target_pairs={{4,0},{8,4},{12,8},{16,12},{20,16},{24,20},{28,24},{0,28},{5,1},{9... | collective-permute-start | bytes 1572872 | tf_op jit(solution)/shard_map/ppermute | solution.py:22
  1071.3 23.1 %collective-permute-start.5 = (f32[4,16,16,128]{3,2,1,0:T(8,128)S(1)}, f32[4,16,16,128]{3,2,1,0:T(8,128)}, u32[]{:S(2)}, u32[]{:S(2)}) collective-permute-start(f32[4,16,16,128]{3,2,1,0:T(8,128)S(1)} %bitcast.241), channel_id=1, source_target_pairs={{0,4},{4,8},{8,12},{12,16},{16,20},{20,24},{24,28},{28,0},{1,5},{5... | collective-permute-start | bytes 1572872 | tf_op jit(solution)/shard_map/ppermute | solution.py:19
  1079.4 15.0 %copy-start.21 = (f32[4,16,15,128]{3,2,1,0:T(8,128)S(1)}, f32[4,16,15,128]{3,2,1,0:T(8,128)}, u32[]{:S(2)}) copy-start(f32[4,16,15,128]{3,2,1,0:T(8,128)} %get-tuple-element.79) | copy-start | bytes 1474564
  1079.4 15.0 %copy-start.22 = (f32[4,16,15,128]{3,2,1,0:T(8,128)S(1)}, f32[4,16,15,128]{3,2,1,0:T(8,128)}, u32[]{:S(2)}) copy-start(f32[4,16,15,128]{3,2,1,0:T(8,128)} %get-tuple-element.80) | copy-start | bytes 1474564
  1079.4 15.0 %copy-start.23 = (f32[4,16,14,128]{3,2,1,0:T(8,128)S(1)}, f32[4,16,14,128]{3,2,1,0:T(8,128)}, u32[]{:S(2)}) copy-start(f32[4,16,14,128]{3,2,1,0:T(8,128)} %get-tuple-element.83) | copy-start | bytes 1376260
  1155.7 38.2 %copy-start.46 = (f32[1,128]{1,0:T(1,128)S(1)}, f32[1,128]{1,0:T(1,128)}, u32[]{:S(2)}) copy-start(f32[1,128]{1,0:T(1,128)} %get-tuple-element.189) | copy-start | bytes 1540
  (39 other events, 315.3 us)
Sparse Core Ops, SparseCore 0:
  9.5 25.5 all-gather.4
  41.9 78.3 all-reduce.7
  121.8 22.4 all-gather.6
  282.0 72.4 all-reduce.9
  398.1 21.4 all-gather.8
  426.4 78.2 all-reduce.11
  680.1 72.7 all-reduce.13
  797.0 21.4 all-gather.10
  825.4 78.3 all-reduce.15
  1079.5 72.6 all-reduce.17
where the time goes:
time: 1210 us; the launch traced here: 1200 us
  waiting for transfers between devices  501 us (41%)
  other arithmetic  387 us (32%)
  blocking collectives  110 us (9%)
  local copies, waits for them, and re-layouts  93.1 us (8%)
  matrix products  77.4 us (6%)
  between operations  22.9 us (2%)
    another operation x44, other arithmetic, local(): factor = jnp.linalg.cholesky(margin)  240 us
    psum x3, waiting for transfers between devices, local(): margin = lax.psum(matmul(gathered.T, gathered), 'grid')  233 us
    psum x3, waiting for transfers between devices, local(): coupling = lax.psum(matmul(every_projector.T, vectors), 'grid')  160 us
    another operation x7, other arithmetic, local(): jax.scipy.linalg.solve_triangular(factor, identity_matrix, lower=True)  125 us
    all_gather x3, waiting for transfers between devices, local(): lax.all_gather(vectors.reshape(grid_shape), 'band', axis=3, tiled=True)  70.3 us
    psum x3, blocking collectives, local(): rayleigh = lax.psum(jnp.sum(vectors * applied, axis=0), 'grid')  58.9 us
    psum x3, blocking collectives, local(): squared = lax.psum(jnp.sum(residual * residual, axis=0), 'grid')  51.4 us
    dot_general x12, matrix products, matmul(): jnp.dot(left, right, precision=HIGHEST, preferred_element_type=jnp.float32)  44.3 us
  transfers between devices with their start and end apart: 16, of which 12 were waited for; matrix products, arithmetic and copies ran while one was open for 16% of the time, Pallas kernels for 0%

commit v1 on v0

--- a/solution.py
+++ b/solution.py
@@ -67,7 +67,11 @@
         inverse = jax.scipy.linalg.solve_triangular(factor, identity_matrix, lower=True)
         transform = inverse.T
         vectors = matmul(gathered, lax.dynamic_slice_in_dim(transform, first_band, local_bands, 1))
-        coupling = lax.psum(matmul(every_projector.T, vectors), "grid")
+
+        def _time_set(view):
+            return jnp.sum(lax.all_gather(view, "grid"), axis=0)
+
+        coupling = _time_set(matmul(every_projector.T, vectors))
         exchange_part = matmul(every_projector, coupling)
         grid_field = vectors.reshape(grid_shape)
         applied = (-0.5 * laplacian(grid_field) + potential[..., None] * grid_field).reshape(

time: 1210 us -> 1130 us (0.934)
  waiting for transfers between devices: 501 us -> 443 us
  local copies, waits for them, and re-layouts: 93.1 us -> 77.8 us
    psum x3 -> x0, waiting for transfers between devices: 160 us -> none  [local(): coupling = lax.psum(matmul(every_projector.T, vectors), 'grid')]
    all_gather x0 -> x3, waiting for transfers between devices: none -> 77.7 us  [_time_set(): return jnp.sum(lax.all_gather(view, 'grid'), axis=0)]
    slice x48, local copies, waits for them, and re-layouts: 35.1 us -> 4.23 us  [laplacian(): jnp.roll(grid_field, distance, dimension)]
    ppermute x3, waiting for transfers between devices: 35.4 us -> 60.6 us  [with_halo(): lax.ppermute(lax.slice_in_dim(block, 0, width, axis=dim), axis, backward)]
  transfers between devices with their start and end apart: 16 -> 16, of which waited for: 12 -> 12; matrix products, arithmetic and copies ran while one was open for 16% -> 15% of each run, Pallas kernels for 0% -> 0%
where the time goes in v1:
time: 1130 us
  waiting for transfers between devices  443 us (39%)
  other arithmetic  387 us (34%)
  blocking collectives  109 us (10%)
  local copies, waits for them, and re-layouts  77.8 us (7%)
  matrix products  77.7 us (7%)
  between operations  23.4 us (2%)
    another operation x44, other arithmetic, local(): factor = jnp.linalg.cholesky(margin)  240 us
    psum x3, waiting for transfers between devices, local(): margin = lax.psum(matmul(gathered.T, gathered), 'grid')  233 us
    another operation x7, other arithmetic, local(): jax.scipy.linalg.solve_triangular(factor, identity_matrix, lower=True)  126 us
    all_gather x3, waiting for transfers between devices, _time_set(): return jnp.sum(lax.all_gather(view, 'grid'), axis=0)  77.7 us
    all_gather x3, waiting for transfers between devices, local(): lax.all_gather(vectors.reshape(grid_shape), 'band', axis=3, tiled=True)  70 us
    ppermute x3, waiting for transfers between devices, with_halo(): lax.ppermute(lax.slice_in_dim(block, 0, width, axis=dim), axis, backward)  60.6 us
    psum x3, blocking collectives, local(): rayleigh = lax.psum(jnp.sum(vectors * applied, axis=0), 'grid')  56.9 us
    psum x3, blocking collectives, local(): squared = lax.psum(jnp.sum(residual * residual, axis=0), 'grid')  52 us
  transfers between devices with their start and end apart: 16, of which 12 were waited for; matrix products, arithmetic and copies ran while one was open for 15% of the time, Pallas kernels for 0%

profile of v1, /device:TPU:0, one launch (start us, length us, event | category | flops | bytes accessed | tf_op | source)
XLA Modules:
  0.0 1128.7 jit_solution(13358649261294858395)
XLA Ops:
  7.9 27.1 %all-gather.11.cloned.1.call-done = f32[4,16,16,512]{3,2,1,0:T(8,128)} async-done(((f32[4,16,16,128]{3,2,1,0:T(8,128)}), f32[4,16,16,512]{3,2,1,0:T(8,128)}) %all-gather.11.cloned.1.call-update) | async-done | bytes 2097168 | tf_op jit(solution)/shard_map/all_gather | solution.py:62
  43.2 77.1 %all-reduce.5.cloned.1.call-done = f32[512,512]{0,1:T(8,128)} async-done(((f32[512,512]{0,1:T(8,128)}), f32[512,512]{0,1:T(8,128)}) %all-reduce.5.cloned.1.call-update) | async-done | bytes 1048592 | tf_op jit(solution)/shard_map/psum | solution.py:65
  218.7 39.3 %custom-call.34 = f32[4,128,128]{1,2,0:T(8,128)S(1)} custom-call(f32[4,128,128]{2,1,0:T(8,128)S(1)} %get-tuple-element.25), custom_call_target="InvertDiagBlocksLowerTriangular" | custom-call | tf_op jit(solution)/shard_map/jit(_solve_triangular)/triangular_solve | solution.py:67
  272.2 19.1 %collective-permute-done = f32[4,16,16,128]{3,2,1,0:T(8,128)S(1)} collective-permute-done((f32[4,16,16,128]{3,2,1,0:T(8,128)S(1)}, f32[4,16,16,128]{3,2,1,0:T(8,128)S(1)}, u32[]{:S(2)}, u32[]{:S(2)}) %collective-permute-start) | collective-permute-done | bytes 524320 | tf_op jit(solution)/shard_map/ppermute | solution.py:22
  296.4 27.5 %all-gather.19.cloned.1.call-done = f32[4096,128]{0,1:T(8,128)} async-done(((f32[512,128]{0,1:T(8,128)}), f32[4096,128]{0,1:T(8,128)}) %all-gather.19.cloned.1.call-update) | async-done | bytes 2097168 | tf_op jit(solution)/shard_map/all_gather | solution.py:72
  331.2 19.0 %psum.64 = f32[128]{0:T(128)S(1)} all-reduce(f32[128]{0:T(128)S(1)} %get-tuple-element.195), channel_id=1, replica_groups=mesh['grid'=8,'band'=4] {'grid'}, use_global_device_ids=true, to_apply=%region_11.14 | all-reduce | flops 128 | bytes 1024 | tf_op jit(solution)/shard_map/psum | solution.py:80
  350.4 17.3 %psum.65 = f32[128]{0:T(128)S(1)} all-reduce(f32[128]{0:T(128)S(1)} %multiply_reduce_fusion.4), channel_id=1, replica_groups=mesh['grid'=8,'band'=4] {'grid'}, use_global_device_ids=true, to_apply=%region_13.16 | all-reduce | flops 128 | bytes 1024 | tf_op jit(solution)/shard_map/psum | solution.py:82
  370.8 21.4 %all-gather.15.cloned.1.call-done = f32[4,16,16,512]{3,2,1,0:T(8,128)} async-done(((f32[4,16,16,128]{3,2,1,0:T(8,128)}), f32[4,16,16,512]{3,2,1,0:T(8,128)}) %all-gather.15.cloned.1.call-update) | async-done | bytes 2097168 | tf_op jit(solution)/shard_map/all_gather | solution.py:62
  399.2 78.2 %all-reduce.7.cloned.1.call-done = f32[512,512]{0,1:T(8,128)} async-done(((f32[512,512]{0,1:T(8,128)}), f32[512,512]{0,1:T(8,128)}) %all-reduce.7.cloned.1.call-update) | async-done | bytes 1048592 | tf_op jit(solution)/shard_map/psum | solution.py:65
  576.6 14.1 %while.7 = (s32[]{:T(128)}, f32[512,512]{1,0:T(8,128)}, s32[4,2]{0,1:T(2,128)S(1)}, f32[4,128,128]{2,1,0:T(8,128)}, s32[]{:T(128)}) while((s32[]{:T(128)}, f32[512,512]{1,0:T(8,128)}, s32[4,2]{0,1:T(2,128)S(1)}, f32[4,128,128]{2,1,0:T(8,128)}, s32[]{:T(128)}) %tuple.160), condition=%wide.while_cond.clone, body=%wide.while_body.clone.sunk | while | flops 2 | bytes 132705 | solution.py:67
  590.8 40.7 %custom-call.38 = f32[4,128,128]{1,2,0:T(8,128)} custom-call(f32[4,128,128]{2,1,0:T(8,128)} %get-tuple-element.26), custom_call_target="InvertDiagBlocksLowerTriangular" | custom-call | tf_op jit(solution)/shard_map/jit(_solve_triangular)/triangular_solve | solution.py:67
  648.3 20.7 %collective-permute-done.2 = f32[4,16,16,128]{3,2,1,0:T(8,128)} collective-permute-done((f32[4,16,16,128]{3,2,1,0:T(8,128)S(1)}, f32[4,16,16,128]{3,2,1,0:T(8,128)}, u32[]{:S(2)}, u32[]{:S(2)}) %collective-permute-start.2) | collective-permute-done | bytes 524320 | tf_op jit(solution)/shard_map/ppermute | solution.py:22
  675.2 25.0 %all-gather.21.cloned.1.call-done = f32[4096,128]{0,1:T(8,128)} async-done(((f32[512,128]{0,1:T(8,128)}), f32[4096,128]{0,1:T(8,128)}) %all-gather.21.cloned.1.call-update) | async-done | bytes 2097168 | tf_op jit(solution)/shard_map/all_gather | solution.py:72
  706.9 19.0 %psum.67 = f32[128]{0:T(128)S(1)} all-reduce(f32[128]{0:T(128)S(1)} %get-tuple-element.199), channel_id=1, replica_groups=mesh['grid'=8,'band'=4] {'grid'}, use_global_device_ids=true, to_apply=%region_17.20 | all-reduce | flops 128 | bytes 1024 | tf_op jit(solution)/shard_map/psum | solution.py:80
  726.1 17.3 %psum.68 = f32[128]{0:T(128)S(1)} all-reduce(f32[128]{0:T(128)S(1)} %multiply_reduce_fusion.2), channel_id=1, replica_groups=mesh['grid'=8,'band'=4] {'grid'}, use_global_device_ids=true, to_apply=%region_19.22 | all-reduce | flops 128 | bytes 1024 | tf_op jit(solution)/shard_map/psum | solution.py:82
  746.5 21.4 %all-gather.17.cloned.1.call-done = f32[4,16,16,512]{3,2,1,0:T(8,128)} async-done(((f32[4,16,16,128]{3,2,1,0:T(8,128)}), f32[4,16,16,512]{3,2,1,0:T(8,128)}) %all-gather.17.cloned.1.call-update) | async-done | bytes 2097168 | tf_op jit(solution)/shard_map/all_gather | solution.py:62
  775.0 78.2 %all-reduce.9.cloned.1.call-done = f32[512,512]{0,1:T(8,128)} async-done(((f32[512,512]{0,1:T(8,128)}), f32[512,512]{0,1:T(8,128)}) %all-reduce.9.cloned.1.call-update) | async-done | bytes 1048592 | tf_op jit(solution)/shard_map/psum | solution.py:65
  933.4 11.7 %cholesky.575 = f32[128,128]{1,0:T(8,128)S(1)} custom-call(f32[128,128]{1,0:T(8,128)S(1)} %convolution_subtract_fusion.15), custom_call_target="Cholesky" | custom-call | tf_op jit(solution)/shard_map/jit(cholesky)/cholesky | solution.py:66
  952.3 14.2 %while.8 = (s32[]{:T(128)}, f32[512,512]{1,0:T(8,128)}, s32[4,2]{0,1:T(2,128)S(1)}, f32[4,128,128]{2,1,0:T(8,128)}, s32[]{:T(128)}) while((s32[]{:T(128)}, f32[512,512]{1,0:T(8,128)}, s32[4,2]{0,1:T(2,128)S(1)}, f32[4,128,128]{2,1,0:T(8,128)}, s32[]{:T(128)}) %tuple.161), condition=%wide.while_cond.clone.1, body=%wide.while_body.clone.1.sunk | while | flops 2 | bytes 132705 | solution.py:67
  966.5 40.7 %custom-call.42 = f32[4,128,128]{1,2,0:T(8,128)} custom-call(f32[4,128,128]{2,1,0:T(8,128)} %get-tuple-element.27), custom_call_target="InvertDiagBlocksLowerTriangular" | custom-call | tf_op jit(solution)/shard_map/jit(_solve_triangular)/triangular_solve | solution.py:67
  1023.9 20.8 %collective-permute-done.4 = f32[4,16,16,128]{3,2,1,0:T(8,128)} collective-permute-done((f32[4,16,16,128]{3,2,1,0:T(8,128)S(1)}, f32[4,16,16,128]{3,2,1,0:T(8,128)}, u32[]{:S(2)}, u32[]{:S(2)}) %collective-permute-start.4) | collective-permute-done | bytes 524320 | tf_op jit(solution)/shard_map/ppermute | solution.py:22
  1050.9 25.2 %all-gather.23.cloned.1.call-done = f32[4096,128]{0,1:T(8,128)} async-done(((f32[512,128]{0,1:T(8,128)}), f32[4096,128]{0,1:T(8,128)}) %all-gather.23.cloned.1.call-update) | async-done | bytes 2097168 | tf_op jit(solution)/shard_map/all_gather | solution.py:72
  1082.7 19.0 %psum.70 = f32[128]{0:T(128)S(1)} all-reduce(f32[128]{0:T(128)S(1)} %get-tuple-element.203), channel_id=1, replica_groups=mesh['grid'=8,'band'=4] {'grid'}, use_global_device_ids=true, to_apply=%region_23.26 | all-reduce | flops 128 | bytes 1024 | tf_op jit(solution)/shard_map/psum | solution.py:80
  1101.9 17.3 %psum.71 = f32[128]{0:T(128)S(1)} all-reduce(f32[128]{0:T(128)S(1)} %multiply_reduce_fusion), channel_id=1, replica_groups=mesh['grid'=8,'band'=4] {'grid'}, use_global_device_ids=true, to_apply=%region_25.28 | all-reduce | flops 128 | bytes 1024 | tf_op jit(solution)/shard_map/psum | solution.py:82
  (315 shorter events, 430.3 us)
Async XLA Ops:
  7.2 27.9 %all-gather.11.cloned.1.call-start = ((), (), s32[]{:S(2)}) async-start(), calls=%async_computation | async-start | bytes 2621440 | tf_op jit(solution)/shard_map/all_gather | solution.py:62
  7.9 112.4 %all-reduce.5.cloned.1.call-start = ((), (), s32[]{:S(2)}) async-start(), calls=%async_computation.1 | async-start | bytes 2097152 | tf_op jit(solution)/shard_map/psum | solution.py:65
  41.9 225.5 %all-gather.13.cloned.1.call-start = ((), (), s32[]{:S(2)}) async-start(), calls=%async_computation.2 | async-start | bytes 2621440 | tf_op jit(solution)/shard_map/all_gather | solution.py:55
  42.6 281.4 %all-gather.19.cloned.1.call-start = ((), (), s32[]{:S(2)}) async-start(), calls=%async_computation.7 | async-start | bytes 2359296 | tf_op jit(solution)/shard_map/all_gather | solution.py:72
  43.2 216.9 %copy-start.4 = (f32[512,512]{1,0:T(8,128)}, f32[512,512]{1,0:T(8,128)S(1)}, u32[]{:S(2)}) copy-start(f32[512,512]{1,0:T(8,128)S(1)} %fusion.6) | copy-start | bytes 3145732
  263.6 27.7 %collective-permute-start = (f32[4,16,16,128]{3,2,1,0:T(8,128)S(1)}, f32[4,16,16,128]{3,2,1,0:T(8,128)S(1)}, u32[]{:S(2)}, u32[]{:S(2)}) collective-permute-start(f32[4,16,16,128]{3,2,1,0:T(8,128)S(1)} %bitcast.268), channel_id=1, source_target_pairs={{4,0},{8,4},{12,8},{16,12},{20,16},{24,20},{28,24},{0,28},{5,1},{9... | collective-permute-start | bytes 1572872 | tf_op jit(solution)/shard_map/ppermute | solution.py:22
  266.6 24.7 %collective-permute-start.1 = (f32[4,16,16,128]{3,2,1,0:T(8,128)S(1)}, f32[4,16,16,128]{3,2,1,0:T(8,128)S(1)}, u32[]{:S(2)}, u32[]{:S(2)}) collective-permute-start(f32[4,16,16,128]{3,2,1,0:T(8,128)S(1)} %bitcast.269), channel_id=1, source_target_pairs={{0,4},{4,8},{8,12},{12,16},{16,20},{20,24},{24,28},{28,0},{1,5},{5... | collective-permute-start | bytes 1572872 | tf_op jit(solution)/shard_map/ppermute | solution.py:19
  270.9 121.3 %all-gather.15.cloned.1.call-start = ((), (), s32[]{:S(2)}) async-start(), calls=%async_computation.3 | async-start | bytes 2621440 | tf_op jit(solution)/shard_map/all_gather | solution.py:62
  272.1 20.1 %copy-start.19 = (f32[4,16,16]{2,1,0:T(8,128)S(1)}, f32[4,16,16]{2,1,0:T(8,128)}, u32[]{:S(2)}) copy-start(f32[4,16,16]{2,1,0:T(8,128)} %param.8) | copy-start | bytes 12292
  272.1 20.1 %copy-start.22 = (f32[4,16,1,128]{3,2,1,0:T(1,128)S(1)}, f32[4,16,1,128]{3,2,1,0:T(1,128)}, u32[]{:S(2)}) copy-start(f32[4,16,1,128]{3,2,1,0:T(1,128)} %get-tuple-element.142) | copy-start | bytes 98308
  370.8 106.6 %all-reduce.7.cloned.1.call-start = ((), (), s32[]{:S(2)}) async-start(), calls=%async_computation.4 | async-start | bytes 2097152 | tf_op jit(solution)/shard_map/psum | solution.py:65
  399.0 301.2 %all-gather.21.cloned.1.call-start = ((), (), s32[]{:S(2)}) async-start(), calls=%async_computation.8 | async-start | bytes 2359296 | tf_op jit(solution)/shard_map/all_gather | solution.py:72
  532.4 99.2 %copy-start.5 = (f32[512,512]{1,0:T(8,128)S(1)}, f32[512,512]{1,0:T(8,128)}, u32[]{:S(2)}) copy-start(f32[512,512]{1,0:T(8,128)} %copy-done.4) | copy-start | bytes 3145732
  641.2 27.8 %collective-permute-start.2 = (f32[4,16,16,128]{3,2,1,0:T(8,128)S(1)}, f32[4,16,16,128]{3,2,1,0:T(8,128)}, u32[]{:S(2)}, u32[]{:S(2)}) collective-permute-start(f32[4,16,16,128]{3,2,1,0:T(8,128)S(1)} %bitcast.230), channel_id=1, source_target_pairs={{4,0},{8,4},{12,8},{16,12},{20,16},{24,20},{28,24},{0,28},{5,1},{9... | collective-permute-start | bytes 1572872 | tf_op jit(solution)/shard_map/ppermute | solution.py:22
  644.2 24.8 %collective-permute-start.3 = (f32[4,16,16,128]{3,2,1,0:T(8,128)S(1)}, f32[4,16,16,128]{3,2,1,0:T(8,128)}, u32[]{:S(2)}, u32[]{:S(2)}) collective-permute-start(f32[4,16,16,128]{3,2,1,0:T(8,128)S(1)} %bitcast.231), channel_id=1, source_target_pairs={{0,4},{4,8},{8,12},{12,16},{16,20},{20,24},{24,28},{28,0},{1,5},{5... | collective-permute-start | bytes 1572872 | tf_op jit(solution)/shard_map/ppermute | solution.py:19
  647.2 120.7 %all-gather.17.cloned.1.call-start = ((), (), s32[]{:S(2)}) async-start(), calls=%async_computation.5 | async-start | bytes 2621440 | tf_op jit(solution)/shard_map/all_gather | solution.py:62
  648.1 20.9 %copy-start.23 = (f32[4,16,1,128]{3,2,1,0:T(1,128)S(1)}, f32[4,16,1,128]{3,2,1,0:T(1,128)}, u32[]{:S(2)}) copy-start(f32[4,16,1,128]{3,2,1,0:T(1,128)} %get-tuple-element.110) | copy-start | bytes 98308
  746.4 106.7 %all-reduce.9.cloned.1.call-start = ((), (), s32[]{:S(2)}) async-start(), calls=%async_computation.6 | async-start | bytes 2097152 | tf_op jit(solution)/shard_map/psum | solution.py:65
  774.7 301.4 %all-gather.23.cloned.1.call-start = ((), (), s32[]{:S(2)}) async-start(), calls=%async_computation.9 | async-start | bytes 2359296 | tf_op jit(solution)/shard_map/all_gather | solution.py:72
  908.2 99.0 %copy-start.6 = (f32[512,512]{1,0:T(8,128)S(1)}, f32[512,512]{1,0:T(8,128)}, u32[]{:S(2)}) copy-start(f32[512,512]{1,0:T(8,128)} %copy-done.4) | copy-start | bytes 3145732
  1007.2 5.3 copy-start.20
  1016.9 27.8 %collective-permute-start.4 = (f32[4,16,16,128]{3,2,1,0:T(8,128)S(1)}, f32[4,16,16,128]{3,2,1,0:T(8,128)}, u32[]{:S(2)}, u32[]{:S(2)}) collective-permute-start(f32[4,16,16,128]{3,2,1,0:T(8,128)S(1)} %bitcast.249), channel_id=1, source_target_pairs={{4,0},{8,4},{12,8},{16,12},{20,16},{24,20},{28,24},{0,28},{5,1},{9... | collective-permute-start | bytes 1572872 | tf_op jit(solution)/shard_map/ppermute | solution.py:22
  1019.9 24.8 %collective-permute-start.5 = (f32[4,16,16,128]{3,2,1,0:T(8,128)S(1)}, f32[4,16,16,128]{3,2,1,0:T(8,128)}, u32[]{:S(2)}, u32[]{:S(2)}) collective-permute-start(f32[4,16,16,128]{3,2,1,0:T(8,128)S(1)} %bitcast.250), channel_id=1, source_target_pairs={{0,4},{4,8},{8,12},{12,16},{16,20},{20,24},{24,28},{28,0},{1,5},{5... | collective-permute-start | bytes 1572872 | tf_op jit(solution)/shard_map/ppermute | solution.py:19
  1023.7 20.9 %copy-start.24 = (f32[4,16,1,128]{3,2,1,0:T(1,128)S(1)}, f32[4,16,1,128]{3,2,1,0:T(1,128)}, u32[]{:S(2)}) copy-start(f32[4,16,1,128]{3,2,1,0:T(1,128)} %get-tuple-element.78) | copy-start | bytes 98308
  (17 other events, 38.3 us)
Sparse Core Ops, SparseCore 0:
  9.5 25.5 all-gather.10
  42.0 78.3 all-reduce.4
  121.9 22.4 all-gather.12
  271.1 52.8 all-gather.18
  370.9 21.2 all-gather.14
  399.1 78.2 all-reduce.6
  647.3 52.8 all-gather.20
  746.5 21.3 all-gather.16
  774.8 78.2 all-reduce.8
  1023.2 52.8 all-gather.22
